TPU v7x, 32 devices: a whole 2x2x4 slice. The times are simulated.
32 devices in a mesh: row: 8 (over z, y), col: 4 (over x, core).
Axes of the slice: x: 2, y: 2, z: 4, core: 2. Of those that a mesh axis runs over, the one named last changes fastest.
Arguments:
- child_parent: int32 [4096], P(('row', 'col')), may hold values from 0 to 1023, as said below
- prefix_len: int32 [4096], P(('row', 'col')), may hold values from 1 to 40
- child_delta: bfloat16 [4096, 3584], P(('row', 'col')), may hold values from -6 to 6
- parent_hidden: bfloat16 [1024, 3584], P(('row', 'col')), may hold values from -6 to 6
- parent_cache: bfloat16 [1024, 2, 2, 128, 128], P(('row', 'col')), may hold values from -720 to 720
- prefix_cache: bfloat16 [32, 2, 2, 5120, 128], P(('row', 'col')), may hold values from -720 to 720
- norm_gain: float32 [3584], replicated, may hold values from 0.1 to 1.9
- w_query: bfloat16 [3584, 1792], replicated, may hold values from -0.09375 to 0.09375
- w_kv: bfloat16 [3584, 512], replicated, may hold values from -0.09375 to 0.09375
Outputs:
- context: bfloat16 [4096, 1792], P(('row', 'col'))
- child_kv: bfloat16 [4096, 512], P(('row', 'col'))
Inputs may be any that keep to these rules, and one draw needn't show every extreme that they name: `child_parent`: each device's 128 children name exactly 32 parents held in each column of devices; the children of any one row of devices name exactly 16 parents held by any one device; one device's children name at most 4 parents held by one device, and exactly 4 for some pairs. Parent p is held by device p // 32, device index = row index * 4 + column index.
All inputs are finite; a program needn't handle non-finite values.
Results may differ from a plain program's by a relative error of at most 0.0085.
The roundings to bfloat16 on the way count: a program that leaves them out, or rounds other values in their place, can miss the bound.
Values may be sent and summed in bfloat16 or wider, within the bound.
No kernel may reach another device: no remote copies, remote signals or barrier semaphores. Data moves between devices by JAX's collectives and lax.ppermute only.
A program may use at most 256 MiB of HBM per device.

v0:
```python
import math

import jax
import jax.numpy as jnp
from jax import lax
from jax.sharding import PartitionSpec as P

EPSILON = 1e-06


def project_rows(parent_rows, delta_rows, norm_gain, w_query, w_kv):
    widened = parent_rows.astype(jnp.float32) + delta_rows.astype(jnp.float32)
    inverse = lax.rsqrt(jnp.mean(widened * widened, axis=-1, keepdims=True) + EPSILON)
    normed = (widened * inverse * norm_gain).astype(jnp.bfloat16)
    queries = jnp.dot(normed, w_query, preferred_element_type=jnp.float32).astype(jnp.bfloat16)
    new_kv = jnp.dot(normed, w_kv, preferred_element_type=jnp.float32).astype(jnp.bfloat16)
    return (queries, new_kv)


def prefix_scores(grouped, block_counts, prefix_rows, block_tokens, scale_factor):
    score_pre = (
        jnp.einsum("chgd,hld->hcgl", grouped, prefix_rows[0], preferred_element_type=jnp.float32)
        * scale_factor
    )
    key_positions = jnp.arange(prefix_rows.shape[2], dtype=jnp.int32)
    limits = block_counts * block_tokens
    in_prefix = key_positions[None, None, None, :] < limits[None, :, None, None]
    return jnp.where(in_prefix, score_pre, -jnp.inf)


def pick_slots(member, rank_grid, values, slot_count):
    wanted = jnp.arange(slot_count, dtype=jnp.int32)
    match_mask = member[..., None, :] & (rank_grid[..., None, :] == wanted[:, None])
    return jnp.sum(jnp.where(match_mask, values[..., None, :], 0), axis=-1)


def direct_layout(
    whole_source, whole_local, my_source, my_device, device_count, per_device, capacity
):
    positions = jnp.arange(per_device, dtype=jnp.int32)
    source_grid = whole_source.reshape(device_count, per_device)
    local_grid = whole_local.reshape(device_count, per_device)
    member = source_grid == my_device
    rank_grid = jnp.cumsum(member.astype(jnp.int32), axis=1) - 1
    send_ids = pick_slots(member, rank_grid, local_grid, capacity)
    earlier = (my_source[None, :] == my_source[:, None]) & (positions[None, :] < positions[:, None])
    my_rank = jnp.sum(earlier.astype(jnp.int32), axis=1)
    return (send_ids, my_source * capacity + my_rank)


def heads_to_rows(stat, child_count):
    return jnp.transpose(stat[..., 0], (1, 0, 2)).reshape(child_count, -1)


def rows_to_heads(stat, child_count, kv_heads):
    return jnp.transpose(stat.reshape(child_count, kv_heads, -1), (1, 0, 2))[..., None]


def local(
    child_parent,
    prefix_len,
    child_delta,
    parent_hidden,
    parent_cache,
    prefix_cache,
    norm_gain,
    w_query,
    w_kv,
):
    row_count = lax.axis_size("row")
    col_count = lax.axis_size("col")
    device_count = row_count * col_count
    my_row = lax.axis_index("row")
    my_col = lax.axis_index("col")
    my_device = my_row * col_count + my_col
    per_device = child_parent.shape[0]
    parent_count = parent_hidden.shape[0]
    whole_map = lax.all_gather(child_parent, ("row", "col"), axis=0, tiled=True)
    whole_source = whole_map // parent_count
    whole_local = whole_map % parent_count
    my_source = child_parent // parent_count
    capacity = 2 * ((per_device // (2 * col_count) + row_count - 1) // row_count)
    send_ids, flat_index = direct_layout(
        whole_source, whole_local, my_source, my_device, device_count, per_device, capacity
    )
    arrived_hidden = lax.all_to_all(
        parent_hidden[send_ids], ("row", "col"), split_axis=0, concat_axis=0, tiled=True
    )
    hidden_rows = arrived_hidden.reshape(-1, arrived_hidden.shape[-1])[flat_index]
    queries, new_kv = project_rows(hidden_rows, child_delta, norm_gain, w_query, w_kv)
    prefix_rows = prefix_cache[0]
    kv_heads = prefix_rows.shape[1]
    head_dim = prefix_rows.shape[-1]
    block_tokens = parent_cache.shape[3]
    scale_factor = 1.0 / math.sqrt(head_dim)
    grouped = queries.reshape(per_device, kv_heads, -1, head_dim)
    score_pre = prefix_scores(grouped, prefix_len, prefix_rows, block_tokens, scale_factor)
    top_pre = jnp.max(score_pre, axis=-1, keepdims=True)
    sum_pre = jnp.sum(jnp.exp(score_pre - top_pre), axis=-1, keepdims=True)
    slot_total = device_count * capacity
    query_box = jnp.zeros((slot_total, queries.shape[1]), jnp.bfloat16).at[flat_index].set(queries)
    top_box = (
        jnp.zeros((slot_total, queries.shape[1] // head_dim), jnp.float32)
        .at[flat_index]
        .set(heads_to_rows(top_pre, per_device))
    )
    sum_box = (
        jnp.zeros((slot_total, queries.shape[1] // head_dim), jnp.float32)
        .at[flat_index]
        .set(heads_to_rows(sum_pre, per_device))
    )
    far_query, far_top, far_sum = (
        lax.all_to_all(
            query_box.reshape(device_count, capacity, -1).astype(jnp.float32),
            ("row", "col"),
            split_axis=0,
            concat_axis=0,
            tiled=True,
        ).astype(jnp.bfloat16),
        lax.all_to_all(
            top_box.reshape(device_count, capacity, -1),
            ("row", "col"),
            split_axis=0,
            concat_axis=0,
            tiled=True,
        ),
        lax.all_to_all(
            sum_box.reshape(device_count, capacity, -1),
            ("row", "col"),
            split_axis=0,
            concat_axis=0,
            tiled=True,
        ),
    )
    own_blocks = parent_cache[send_ids.reshape(-1)]
    item_query = far_query.reshape(slot_total, kv_heads, -1, head_dim)
    score_par = (
        jnp.einsum(
            "chgd,chtd->hcgt", item_query, own_blocks[:, 0], preferred_element_type=jnp.float32
        )
        * scale_factor
    )
    remote_top = rows_to_heads(far_top, slot_total, kv_heads)
    remote_sum = rows_to_heads(far_sum, slot_total, kv_heads)
    joint_top = jnp.maximum(remote_top, jnp.max(score_par, axis=-1, keepdims=True))
    exp_par = jnp.exp(score_par - joint_top)
    joint_sum = remote_sum * jnp.exp(remote_top - joint_top) + jnp.sum(
        exp_par, axis=-1, keepdims=True
    )
    weight_par = (exp_par / joint_sum).astype(jnp.bfloat16)
    share = jnp.einsum(
        "hcgt,chtd->chgd", weight_par, own_blocks[:, 1], preferred_element_type=jnp.float32
    )
    back_share, back_top, back_sum = (
        lax.all_to_all(
            share.reshape(device_count, capacity, -1),
            ("row", "col"),
            split_axis=0,
            concat_axis=0,
            tiled=True,
        ),
        lax.all_to_all(
            heads_to_rows(joint_top, slot_total).reshape(device_count, capacity, -1),
            ("row", "col"),
            split_axis=0,
            concat_axis=0,
            tiled=True,
        ),
        lax.all_to_all(
            heads_to_rows(joint_sum, slot_total).reshape(device_count, capacity, -1),
            ("row", "col"),
            split_axis=0,
            concat_axis=0,
            tiled=True,
        ),
    )
    child_share = back_share.reshape(slot_total, -1)[flat_index]
    child_top = rows_to_heads(back_top.reshape(slot_total, -1)[flat_index], per_device, kv_heads)
    child_sum = rows_to_heads(back_sum.reshape(slot_total, -1)[flat_index], per_device, kv_heads)
    weight_pre = (jnp.exp(score_pre - child_top) / child_sum).astype(jnp.bfloat16)
    context = jnp.einsum(
        "hcgl,hld->chgd", weight_pre, prefix_rows[1], preferred_element_type=jnp.float32
    )
    context = context + child_share.reshape(context.shape)
    return (context.reshape(per_device, -1).astype(jnp.bfloat16), new_kv)


def solution(mesh):
    return jax.shard_map(
        local,
        mesh=mesh,
        in_specs=(
            P(("row", "col")),
            P(("row", "col")),
            P(("row", "col"), None),
            P(("row", "col"), None),
            P(("row", "col"), None, None, None, None),
            P(("row", "col"), None, None, None, None),
            P(),
            P(),
            P(),
        ),
        out_specs=(P(("row", "col"), None), P(("row", "col"), None)),
        check_vma=False,
    )
```

profile of v0, /device:TPU:0, one launch (start us, length us, event | category | flops | bytes accessed | tf_op | source)
XLA Modules:
  0.0 243.4 jit_solution(16490060737873463714)
XLA Ops:
  0.7 43.6 %all-gather = s32[32,1,128]{2,1,0:T(1,128)S(1)} all-gather(s32[1,1,128]{2,1,0:T(1,128)} %bitcast.109), channel_id=1, replica_groups=mesh['row'=8,'col'=4] {'row','col'}, dimensions={0}, use_global_device_ids=true | all-gather | bytes 16896 | tf_op jit(solution)/shard_map/all_gather | solution.py:78
  47.3 2.6 %all-to-all-start = ((bf16[32,4,3584]{2,1,0:T(4,128)(2,1)}), bf16[32,4,3584]{2,1,0:T(4,128)(2,1)S(1)}, u32[]{:S(2)}, u32[]{:S(2)}) async-start(bf16[32,4,3584]{2,1,0:T(4,128)(2,1)} %reshape.190), calls=%async_computation | async-start | bytes 1835008 | tf_op jit(solution)/shard_map/all_to_all | solution.py:86
  50.6 22.7 %all-to-all-done = bf16[32,4,3584]{2,1,0:T(4,128)(2,1)S(1)} async-done(((bf16[32,4,3584]{2,1,0:T(4,128)(2,1)}), bf16[32,4,3584]{2,1,0:T(4,128)(2,1)S(1)}, u32[]{:S(2)}, u32[]{:S(2)}) %all-to-all-start) | async-done | bytes 917536 | tf_op jit(solution)/shard_map/all_to_all | solution.py:86
  76.2 6.9 %convolution_convert_fusion = bf16[128,1792]{1,0:T(8,128)(2,1)S(1)} fusion(bf16[3584,1792]{1,0:T(8,128)(2,1)} %param.16, bf16[128,3584]{1,0:T(8,128)(2,1)} %param.11, bf16[128,3584]{1,0:T(8,128)(2,1)S(1)} %gather_fusion.1, f32[3584]{0:T(1024)S(1)} %copy-done.3, f32[128]{0:T(128)S(1)} %add_rsqrt_fusion), kind=kOutput, calls=%fused_computation.24 | convolution fusion | flops 1647149056 | bytes 15153664 | tf_op jit(solution)/shard_map/dot_general | solution.py:15
  83.4 16.7 %fusion = (f32[2,128,7]{1,2,0:T(8,128)S(1)}, f32[2,128,7,5120]{3,1,2,0:T(8,128)}) fusion(pred[128,5120]{1,0:T(8,128)(4,1)S(1)} %iota_compare_fusion, bf16[128,2,7,128]{0,3,2,1:T(8,128)(2,1)S(1)} %bitcast.100, bf16[1,2,2,5120,128]{4,3,2,1,0:T(8,128)(2,1)} %param.14), kind=kOutput, calls=%fused_computation.12 | convolution fusion | flops 2376333568 | bytes 40442880 | tf_op jit(solution)/shard_map/chgd,hld->hcgl/dot_general | solution.py:22
  100.1 16.8 %exponential_reduce_fusion = f32[2,128,7]{1,2,0:T(8,128)S(1)} fusion(f32[2,128,7,5120]{3,1,2,0:T(8,128)} %get-tuple-element.19, f32[2,128,7]{1,2,0:T(8,128)S(1)} %get-tuple-element.18, pred[128,5120]{1,0:T(8,128)(4,1)S(1)} %iota_compare_fusion), kind=kLoop, calls=%fused_computation.10 | loop fusion | flops 36698368 | bytes 37369856 | tf_op jit(solution)/shard_map/reduce_sum | solution.py:99
  118.5 3.5 %all-to-all-start.4 = ((f32[32,4,14]{2,1,0:T(4,128)}), f32[32,4,14]{2,1,0:T(4,128)S(1)}, u32[]{:S(2)}, u32[]{:S(2)}) async-start(f32[32,4,14]{2,1,0:T(4,128)} %bitcast.17), calls=%async_computation.4 | async-start | bytes 131072 | tf_op jit(solution)/shard_map/all_to_all | solution.py:127
  123.6 5.8 %all-to-all-done.4 = f32[32,4,14]{2,1,0:T(4,128)S(1)} async-done(((f32[32,4,14]{2,1,0:T(4,128)}), f32[32,4,14]{2,1,0:T(4,128)S(1)}, u32[]{:S(2)}, u32[]{:S(2)}) %all-to-all-start.4) | async-done | bytes 7200 | tf_op jit(solution)/shard_map/all_to_all | solution.py:127
  129.4 2.8 %all-to-all-start.1 = ((f32[32,4,14]{2,1,0:T(4,128)}), f32[32,4,14]{2,1,0:T(4,128)S(1)}, u32[]{:S(2)}, u32[]{:S(2)}) async-start(f32[32,4,14]{2,1,0:T(4,128)} %bitcast.10), calls=%async_computation.1 | async-start | bytes 131072 | tf_op jit(solution)/shard_map/all_to_all | solution.py:120
  134.5 4.9 %all-to-all-done.1 = f32[32,4,14]{2,1,0:T(4,128)S(1)} async-done(((f32[32,4,14]{2,1,0:T(4,128)}), f32[32,4,14]{2,1,0:T(4,128)S(1)}, u32[]{:S(2)}, u32[]{:S(2)}) %all-to-all-start.1) | async-done | bytes 7200 | tf_op jit(solution)/shard_map/all_to_all | solution.py:120
  139.4 2.6 %all-to-all-start.2 = ((bf16[32,4,1792]{2,1,0:T(4,128)(2,1)}), bf16[32,4,1792]{2,1,0:T(4,128)(2,1)S(1)}, u32[]{:S(2)}, u32[]{:S(2)}) async-start(bf16[32,4,1792]{2,1,0:T(4,128)(2,1)} %reshape.188), calls=%async_computation.2 | async-start | bytes 917504 | tf_op jit(solution)/shard_map/all_to_all | solution.py:113
  142.3 10.6 %gather_fusion.2 = bf16[128,2,2,128,128]{4,3,2,1,0:T(8,128)(2,1)} fusion(bf16[32,2,2,128,128]{4,3,2,1,0:T(8,128)(2,1)} %param.13, s32[1024]{0:T(1024)S(1)} %pad_clamp_fusion), kind=kCustom, calls=%fused_computation.2 | custom fusion | bytes 33554944 | tf_op jit(solution)/shard_map/gather | solution.py:135
  153.3 3.1 %all-to-all-done.2 = bf16[32,4,1792]{2,1,0:T(4,128)(2,1)S(1)} async-done(((bf16[32,4,1792]{2,1,0:T(4,128)(2,1)}), bf16[32,4,1792]{2,1,0:T(4,128)(2,1)S(1)}, u32[]{:S(2)}, u32[]{:S(2)}) %all-to-all-start.2) | async-done | bytes 458784 | tf_op jit(solution)/shard_map/all_to_all | solution.py:113
  157.6 9.0 %fusion.42 = (f32[2,128,7]{2,1,0:T(8,128)S(1)}, f32[2,128,7,128]{3,2,1,0:T(8,128)}) fusion(bf16[128,2,7,128]{3,2,1,0:T(8,128)(2,1)} %reshape.176, bf16[128,2,2,128,128]{4,3,2,1,0:T(8,128)(2,1)} %gather_fusion.2), kind=kOutput, calls=%fused_computation.85 | convolution fusion | flops 59177216 | bytes 9837568 | tf_op jit(solution)/shard_map/chgd,chtd->hcgt/dot_general | solution.py:138
  166.7 1.9 fusion.19
  169.6 2.7 %all-to-all-start.3 = ((f32[32,4,14]{2,1,0:T(4,128)}), f32[32,4,14]{2,1,0:T(4,128)S(1)}, u32[]{:S(2)}, u32[]{:S(2)}) async-start(f32[32,4,14]{2,1,0:T(4,128)} %reshape_reshape.6), calls=%async_computation.3 | async-start | bytes 131072 | tf_op jit(solution)/shard_map/all_to_all | solution.py:162
  173.3 6.4 %all-to-all-done.3 = f32[32,4,14]{2,1,0:T(4,128)S(1)} async-done(((f32[32,4,14]{2,1,0:T(4,128)}), f32[32,4,14]{2,1,0:T(4,128)S(1)}, u32[]{:S(2)}, u32[]{:S(2)}) %all-to-all-start.3) | async-done | bytes 7200 | tf_op jit(solution)/shard_map/all_to_all | solution.py:162
  179.7 2.6 %all-to-all-start.5 = ((f32[32,4,14]{2,1,0:T(4,128)}), f32[32,4,14]{2,1,0:T(4,128)S(1)}, u32[]{:S(2)}, u32[]{:S(2)}) async-start(f32[32,4,14]{2,1,0:T(4,128)} %reshape_reshape.7), calls=%async_computation.5 | async-start | bytes 131072 | tf_op jit(solution)/shard_map/all_to_all | solution.py:169
  182.3 7.0 %fusion.2 = f32[128,2,7,128]{3,2,1,0:T(8,128)} fusion(bf16[128,2,2,128,128]{4,3,2,1,0:T(8,128)(2,1)} %gather_fusion.2, f32[2,128,7,128]{3,2,1,0:T(8,128)} %get-tuple-element.17, f32[2,128,7]{2,1,0:T(8,128)S(1)} %fusion.24, f32[2,128,7]{2,1,0:T(8,128)S(1)} %bitcast_maximum_fusion), kind=kOutput, calls=%fused_computation.15 | convolution fusion | flops 59408384 | bytes 10369024 | tf_op jit(solution)/shard_map/hcgt,chtd->chgd/dot_general | solution.py:151
  189.4 2.5 %reshape.185 = f32[32,4,1792]{2,1,0:T(4,128)} reshape(f32[128,2,7,128]{3,2,1,0:T(8,128)} %fusion.2) | data formatting | bytes 1835008 | tf_op jit(solution)/shard_map/reshape | solution.py:156
  191.9 6.2 %all-to-all-start.6 = ((f32[32,4,1792]{2,1,0:T(4,128)}), f32[32,4,1792]{2,1,0:T(4,128)}, u32[]{:S(2)}, u32[]{:S(2)}) async-start(f32[32,4,1792]{2,1,0:T(4,128)} %reshape.185), calls=%async_computation.6 | async-start | bytes 1835008 | tf_op jit(solution)/shard_map/all_to_all | solution.py:155
  198.1 3.4 %convolution_convert_fusion.1 = bf16[128,512]{1,0:T(8,128)(2,1)} fusion(bf16[3584,512]{1,0:T(8,128)(2,1)} %param.17, bf16[128,3584]{1,0:T(8,128)(2,1)S(1)} %copy-done.2, bf16[128,3584]{1,0:T(8,128)(2,1)S(1)} %gather_fusion.1, f32[3584]{0:T(1024)S(1)} %copy-done.3, f32[128]{0:T(128)S(1)} %add_rsqrt_fusion), kind=kOutput, calls=%fused_computation.32 | convolution fusion | flops 472580096 | bytes 5650944 | tf_op jit(solution)/shard_map/dot_general | solution.py:16
  202.9 18.3 %all-to-all-done.6 = f32[32,4,1792]{2,1,0:T(4,128)} async-done(((f32[32,4,1792]{2,1,0:T(4,128)}), f32[32,4,1792]{2,1,0:T(4,128)}, u32[]{:S(2)}, u32[]{:S(2)}) %all-to-all-start.6) | async-done | bytes 917536 | tf_op jit(solution)/shard_map/all_to_all | solution.py:155
  224.0 18.4 %fusion.16 = bf16[128,2,7,128]{0,3,2,1:T(8,128)(2,1)S(1)} fusion(f32[128,2,7,128]{0,3,2,1:T(8,128)S(1)} %bitcast.101, bf16[1,2,2,5120,128]{4,3,2,1,0:T(8,128)(2,1)} %param.14, f32[2,128,7,5120]{3,1,2,0:T(8,128)} %get-tuple-element.19, f32[2,128,7]{1,2,0:T(8,128)S(1)} %bitcast.108, f32[2,128,7]{1,2,0:T(8,128)S(1)} %bitcast.107, ...), kind=kOutput, calls=%fused_computation.31 | convolution fusion | flops 2395144192 | bytes 41367552 | tf_op jit(solution)/shard_map/hcgl,hld->chgd/dot_general | solution.py:181
  (71 shorter events, 21.2 us)
Async XLA Ops:
  0.6 44.4 %copy-start = (bf16[32,3584]{1,0:T(8,128)(2,1)S(1)}, bf16[32,3584]{1,0:T(8,128)(2,1)}, u32[]{:S(2)}) copy-start(bf16[32,3584]{1,0:T(8,128)(2,1)} %param.12) | copy-start | bytes 688132
  0.6 49.3 %copy-start.4 = (s32[128]{0:T(128)S(1)}, s32[128]{0:T(128)}, u32[]{:S(2)}) copy-start(s32[128]{0:T(128)} %param.9) | copy-start | bytes 1540
  0.7 49.5 %copy-start.5 = (s32[128]{0:T(128)S(1)}, s32[128]{0:T(128)}, u32[]{:S(2)}) copy-start(s32[128]{0:T(128)} %param.10) | copy-start | bytes 1540
  46.1 30.1 %copy-start.3 = (f32[3584]{0:T(1024)S(1)}, f32[3584]{0:T(1024)}, u32[]{:S(2)}) copy-start(f32[3584]{0:T(1024)} %param.15) | copy-start | bytes 43012
  47.3 26.0 %all-to-all-start = ((bf16[32,4,3584]{2,1,0:T(4,128)(2,1)}), bf16[32,4,3584]{2,1,0:T(4,128)(2,1)S(1)}, u32[]{:S(2)}, u32[]{:S(2)}) async-start(bf16[32,4,3584]{2,1,0:T(4,128)(2,1)} %reshape.190), calls=%async_computation | async-start | bytes 1835008 | tf_op jit(solution)/shard_map/all_to_all | solution.py:86
  118.5 11.0 %all-to-all-start.4 = ((f32[32,4,14]{2,1,0:T(4,128)}), f32[32,4,14]{2,1,0:T(4,128)S(1)}, u32[]{:S(2)}, u32[]{:S(2)}) async-start(f32[32,4,14]{2,1,0:T(4,128)} %bitcast.17), calls=%async_computation.4 | async-start | bytes 131072 | tf_op jit(solution)/shard_map/all_to_all | solution.py:127
  129.4 10.0 %all-to-all-start.1 = ((f32[32,4,14]{2,1,0:T(4,128)}), f32[32,4,14]{2,1,0:T(4,128)S(1)}, u32[]{:S(2)}, u32[]{:S(2)}) async-start(f32[32,4,14]{2,1,0:T(4,128)} %bitcast.10), calls=%async_computation.1 | async-start | bytes 131072 | tf_op jit(solution)/shard_map/all_to_all | solution.py:120
  139.4 17.0 %all-to-all-start.2 = ((bf16[32,4,1792]{2,1,0:T(4,128)(2,1)}), bf16[32,4,1792]{2,1,0:T(4,128)(2,1)S(1)}, u32[]{:S(2)}, u32[]{:S(2)}) async-start(bf16[32,4,1792]{2,1,0:T(4,128)(2,1)} %reshape.188), calls=%async_computation.2 | async-start | bytes 917504 | tf_op jit(solution)/shard_map/all_to_all | solution.py:113
  169.6 10.1 %all-to-all-start.3 = ((f32[32,4,14]{2,1,0:T(4,128)}), f32[32,4,14]{2,1,0:T(4,128)S(1)}, u32[]{:S(2)}, u32[]{:S(2)}) async-start(f32[32,4,14]{2,1,0:T(4,128)} %reshape_reshape.6), calls=%async_computation.3 | async-start | bytes 131072 | tf_op jit(solution)/shard_map/all_to_all | solution.py:162
  172.3 25.7 %copy-start.2 = (bf16[128,3584]{1,0:T(8,128)(2,1)S(1)}, bf16[128,3584]{1,0:T(8,128)(2,1)}, u32[]{:S(2)}) copy-start(bf16[128,3584]{1,0:T(8,128)(2,1)} %param.11) | copy-start | bytes 2752516
  179.7 12.2 %all-to-all-start.5 = ((f32[32,4,14]{2,1,0:T(4,128)}), f32[32,4,14]{2,1,0:T(4,128)S(1)}, u32[]{:S(2)}, u32[]{:S(2)}) async-start(f32[32,4,14]{2,1,0:T(4,128)} %reshape_reshape.7), calls=%async_computation.5 | async-start | bytes 131072 | tf_op jit(solution)/shard_map/all_to_all | solution.py:169
  191.9 29.3 %all-to-all-start.6 = ((f32[32,4,1792]{2,1,0:T(4,128)}), f32[32,4,1792]{2,1,0:T(4,128)}, u32[]{:S(2)}, u32[]{:S(2)}) async-start(f32[32,4,1792]{2,1,0:T(4,128)} %reshape.185), calls=%async_computation.6 | async-start | bytes 1835008 | tf_op jit(solution)/shard_map/all_to_all | solution.py:155
  224.0 19.4 %copy-start.1 = (bf16[32,3584]{1,0:T(8,128)(2,1)S(1)}, bf16[32,3584]{1,0:T(8,128)(2,1)}, u32[]{:S(2)}) copy-start(bf16[32,3584]{1,0:T(8,128)(2,1)} %param.12) | copy-start | bytes 688132
where the time goes:
time: 244 us; the launch traced here: 243 us
  waiting for transfers between devices  61.4 us (25%)
  matrix products  61.4 us (25%)
  blocking collectives  43.6 us (18%)
  local copies, waits for them, and re-layouts  31.6 us (13%)
  starting transfers between devices  23 us (9%)
  other arithmetic  21.4 us (9%)
    all_gather x1, blocking collectives, local(): whole_map = lax.all_gather(child_parent, ('row', 'col'), axis=0, tiled=True)  43.6 us
    all_to_all x1, waiting for transfers between devices, local(): lax.all_to_all(parent_hidden[send_ids], ('row', 'col'), split_axis=0, con...  22.7 us
    dot_general x1, matrix products, local(): jnp.einsum('hcgl,hld->chgd', weight_pre, prefix_rows[1], preferred_elemen...  18.4 us
    all_to_all x1, waiting for transfers between devices, local(): lax.all_to_all(share.reshape(device_count, capacity, -1), ('row', 'col'),...  18.3 us
    reduce_sum x1, other arithmetic, local(): sum_pre = jnp.sum(jnp.exp(score_pre - top_pre), axis=-1, keepdims=True)  16.8 us
    dot_general x1, matrix products, prefix_scores(): jnp.einsum('chgd,hld->hcgl', grouped, prefix_rows[0], preferred_element_t...  16.7 us
    gather x1, local copies, waits for them, and re-layouts, local(): own_blocks = parent_cache[send_ids.reshape(-1)]  10.6 us
    dot_general x1, matrix products, local(): jnp.einsum('chgd,chtd->hcgt', item_query, own_blocks[:, 0], preferred_ele...  9.04 us
  transfers between devices with their start and end apart: 7, of which 6 were waited for; matrix products, arithmetic and copies ran while one was open for 13% of the time, Pallas kernels for 0%

commit v1 on v0

v1 whole, which is shorter than its diff:
```python
import functools
import math

import jax
import jax.numpy as jnp
from jax import lax
from jax.experimental import pallas as pl
from jax.experimental.pallas import tpu as pltpu
from jax.sharding import PartitionSpec as P

EPSILON = 1e-06
LOG2E = 1.4426950408889634
LOW = -1e30
CHILD_TILE = 32
CHUNK = 512
SLOT_UNROLL = 8

f32 = jnp.float32
bf16 = jnp.bfloat16
i32 = jnp.int32
VMEM = pl.BlockSpec(memory_space=pltpu.VMEM)
SMEM = pl.BlockSpec(memory_space=pltpu.SMEM)


def dot(a, b):
    return jnp.dot(a, b, preferred_element_type=f32)


def dot_nt(a, b):
    return lax.dot_general(a, b, (((1,), (1,)), ((), ())), preferred_element_type=f32)


def iota(shape, axis):
    return lax.broadcasted_iota(i32, shape, axis)


def onehot(mask):
    return jnp.where(mask, 1.0, 0.0).astype(bf16)


def to_column(row):
    n = row.shape[1]
    same = iota((n, n), 0) == iota((n, n), 1)
    return jnp.sum(jnp.where(same, jnp.broadcast_to(row, (n, n)), 0.0), axis=1, keepdims=True)


def box_rows(rows, parts, capacity):
    r = iota((rows, 1), 0)
    shift = (parts * capacity).bit_length() - 1
    device = lax.shift_right_logical(r, shift)
    within = lax.bitwise_and(r, parts * capacity - 1)
    part = lax.shift_right_logical(within, capacity.bit_length() - 1)
    rank = lax.bitwise_and(within, capacity - 1)
    return device * capacity + rank, part


def pack_matrix(rows, parts, capacity, slot_row):
    slot, part = box_rows(rows, parts, capacity)
    return jnp.concatenate(
        [onehot((slot_row == slot) & (part == p)) for p in range(parts)], axis=1
    )


def stack_parts(x, parts):
    width = x.shape[1] // parts
    return jnp.concatenate([x[:, p * width : (p + 1) * width] for p in range(parts)], axis=0)


def pack_kernel(parents, capacity, parts, slots, cp_ref, len_ref, delta_ref, box_ref, idx_ref, ids_ref):
    n = cp_ref.shape[1]
    ri, ci = iota((n, n), 0), iota((n, n), 1)
    cp = cp_ref[...].astype(f32)
    src = jnp.floor((cp + 0.5) * (1.0 / parents))
    loc = cp - src * parents
    src_col = to_column(src)
    rank = jnp.sum(jnp.where((src_col == src) & (ri < ci), 1.0, 0.0), axis=0, keepdims=True)
    slot = src * capacity + rank
    rows = box_ref.shape[0]
    pack = pack_matrix(rows, parts, capacity, slot.astype(i32))
    box_ref[...] = dot(pack, stack_parts(delta_ref[...], parts)).astype(bf16)

    slot_col = to_column(slot)
    loc_col = to_column(loc)
    ids_ref[...] = jnp.sum(
        jnp.where(slot_col == iota((n, slots), 1).astype(f32), loc_col, 0.0), axis=0, keepdims=True
    ).astype(i32)
    length = len_ref[...].astype(f32)
    len_col = to_column(length)
    srank = jnp.sum(
        jnp.where((len_col > length) | ((len_col == length) & (ri < ci)), 1.0, 0.0),
        axis=0,
        keepdims=True,
    )
    chosen = to_column(srank) == ci.astype(f32)
    sorted_slot = jnp.sum(jnp.where(chosen, slot_col, 0.0), axis=0, keepdims=True)
    sorted_len = jnp.sum(jnp.where(chosen, len_col, 0.0), axis=0, keepdims=True)
    device = jnp.floor((sorted_slot + 0.5) * (1.0 / capacity))
    base = device * (2 * capacity) + (sorted_slot - device * capacity)
    idx_ref[...] = jnp.concatenate(
        [base, sorted_len, srank, jnp.zeros((5, n), f32)], axis=0
    ).astype(i32)


def project_kernel(
    capacity, parts, box_ref, ids_ref, hidden_ref, gain_ref, wq_ref, wkv_ref, q_ref, qbox_ref, kv_ref, h_ref, n_ref
):
    slots = q_ref.shape[0]
    parents = hidden_ref.shape[0]
    rows, width = box_ref.shape
    features = hidden_ref.shape[1]
    ids_col = to_column(ids_ref[...].astype(f32)).astype(i32)
    pick = onehot(ids_col == iota((slots, parents), 1))
    s = iota((slots, 1), 0)
    base = (
        lax.shift_right_logical(s, capacity.bit_length() - 1) * (parts * capacity)
        + lax.bitwise_and(s, capacity - 1)
    )
    squares = jnp.zeros((slots, 1), f32)
    for p in range(parts):
        take = onehot(iota((slots, rows), 1) == base + p * capacity)
        cols = slice(p * width, (p + 1) * width)
        h = dot(pick, hidden_ref[:, cols]) + dot(take, box_ref[...])
        h_ref[:, cols] = h
        squares = squares + jnp.sum(h * h, axis=1, keepdims=True)
    inverse = lax.rsqrt(squares * (1.0 / features) + EPSILON)
    n_ref[...] = (h_ref[...] * inverse * gain_ref[...]).astype(bf16)
    step = 256
    for j in range(0, q_ref.shape[1], step):
        q_ref[:, j : j + step] = dot(n_ref[...], wq_ref[:, j : j + step]).astype(bf16)
    for j in range(0, kv_ref.shape[1], step):
        kv_ref[:, j : j + step] = dot(n_ref[...], wkv_ref[:, j : j + step]).astype(bf16)
    slot_row = iota((1, slots), 1)
    pack = pack_matrix(qbox_ref.shape[0], 2, capacity, slot_row)
    qbox_ref[...] = dot(pack, stack_parts(q_ref[...], 2)).astype(bf16)


def parent_kernel(capacity, scale, ids_ref, q_ref, kv_ref, cache_ref, out_ref, qs_ref, os_ref, ls_ref):
    slots, width = q_ref.shape
    head_dim = cache_ref.shape[-1]
    kv_heads = cache_ref.shape[2]
    group = width // (kv_heads * head_dim)
    for g in range(kv_heads):
        for h in range(group):
            c0 = (g * group + h) * head_dim
            qs_ref[g, pl.ds(h, slots, stride=8), :] = q_ref[:, c0 : c0 + head_dim].astype(f32)
        qs_ref[g, pl.ds(group, slots, stride=8), :] = jnp.zeros((slots, head_dim), f32)

    def step(i, carry):
        for u in range(SLOT_UNROLL):
            s = i * SLOT_UNROLL + u
            parent = ids_ref[0, s]
            at = pl.ds(pl.multiple_of(s * 8, 8), 8)
            for g in range(kv_heads):
                q = qs_ref[g, at, :].astype(bf16)
                score = dot_nt(q, cache_ref[parent, 0, g]) * scale
                top = jnp.max(score, axis=1, keepdims=True)
                e = jnp.exp(score - top)
                total = jnp.sum(e, axis=1, keepdims=True)
                o = dot(e.astype(bf16), cache_ref[parent, 1, g])
                os_ref[g, at, :] = o / total
                ls_ref[g, at, :] = jnp.broadcast_to(top + jnp.log(total), (8, head_dim))
        return carry

    lax.fori_loop(0, slots // SLOT_UNROLL, step, 0)
    lane = iota((slots, head_dim), 1)
    halves = []
    kv_width = kv_ref.shape[1] // kv_heads
    for g in range(kv_heads):
        pieces = []
        stat = jnp.zeros((slots, head_dim), f32)
        for h in range(group):
            pieces.append(os_ref[g, pl.ds(h, slots, stride=8), :].astype(bf16))
            stat = jnp.where(
                lax.bitwise_and(lane, 15) == h, ls_ref[g, pl.ds(h, slots, stride=8), :], stat
            )
        high = stat.astype(bf16).astype(f32)
        rest = stat - high
        middle = rest.astype(bf16).astype(f32)
        low = rest - middle
        pieces.append(kv_ref[:, g * kv_width : (g + 1) * kv_width])
        pieces.append(jnp.where(lane < 16, high, jnp.where(lane < 32, middle, low)).astype(bf16))
        halves.append(jnp.concatenate(pieces, axis=1))
    pack = pack_matrix(out_ref.shape[0], kv_heads, capacity, iota((1, slots), 1))
    out_ref[...] = dot(pack, jnp.concatenate(halves, axis=0)).astype(bf16)


def prefix_kernel(capacity, scale, block, idx_smem, idx_ref, qbox_ref, cache_ref, o_ref, lse_ref, qs_ref, acc_ref, m_ref, l_ref):
    children = idx_ref.shape[1]
    rows, width = qbox_ref.shape
    head_dim = cache_ref.shape[-1]
    kv_heads = cache_ref.shape[1]
    group = width // head_dim
    tiles = children // CHILD_TILE
    tile_rows = CHILD_TILE * group
    per_chunk = CHUNK // block
    base_col = to_column(idx_ref[0:1, :].astype(f32)).astype(i32)
    len_col = to_column(idx_ref[1:2, :].astype(f32)).astype(i32)
    for g in range(kv_heads):
        take = onehot(iota((children, rows), 1) == base_col + g * capacity)
        q = dot(take, qbox_ref[...]).astype(bf16)
        for t in range(tiles):
            for h in range(group):
                at = t * tile_rows + h * CHILD_TILE
                qs_ref[g, at : at + CHILD_TILE, :] = q[
                    t * CHILD_TILE : (t + 1) * CHILD_TILE, h * head_dim : (h + 1) * head_dim
                ]

    for t in range(tiles):
        at = slice(t * tile_rows, (t + 1) * tile_rows)
        lens = jnp.broadcast_to(len_col[t * CHILD_TILE : (t + 1) * CHILD_TILE], (CHILD_TILE, head_dim))
        lens = jnp.concatenate([lens] * group, axis=0)
        longest = idx_smem[1, t * CHILD_TILE]
        for g in range(kv_heads):
            acc_ref[g] = jnp.zeros((tile_rows, head_dim), f32)
            m_ref[g] = jnp.full((tile_rows, head_dim), LOW, f32)
            l_ref[g] = jnp.zeros((tile_rows, head_dim), f32)

        def step(j, carry):
            keys = pl.ds(pl.multiple_of(j * CHUNK, CHUNK), CHUNK)
            for g in range(kv_heads):
                score = dot_nt(qs_ref[g, at, :], cache_ref[0, g, keys, :])
                parts = []
                for b in range(per_chunk):
                    piece = score[:, b * block : (b + 1) * block] * scale
                    parts.append(jnp.where(lens > j * per_chunk + b, piece, LOW))
                top = functools.reduce(jnp.maximum, parts)
                old = m_ref[g]
                new = jnp.maximum(old, jnp.max(top, axis=1, keepdims=True))
                alpha = jnp.exp2(old - new)
                parts = [jnp.exp2(piece - new) for piece in parts]
                m_ref[g] = new
                l_ref[g] = l_ref[g] * alpha + functools.reduce(jnp.add, parts)
                e = jnp.concatenate([piece.astype(bf16) for piece in parts], axis=1)
                acc_ref[g] = acc_ref[g] * alpha + dot(e, cache_ref[1, g, keys, :])
            return carry

        lax.fori_loop(0, (longest + per_chunk - 1) // per_chunk, step, 0)
        for g in range(kv_heads):
            total = jnp.sum(l_ref[g], axis=1, keepdims=True)
            o_ref[g, at, :] = acc_ref[g] * (1.0 / total)
            lse_ref[g, at, :] = m_ref[g] * (1.0 / LOG2E) + jnp.log(total)


def merge_kernel(capacity, idx_ref, box_ref, o_ref, lse_ref, ctx_ref, kv_ref):
    children = idx_ref.shape[1]
    rows = box_ref.shape[0]
    kv_heads, _, head_dim = o_ref.shape
    group = o_ref.shape[1] // children
    tiles = children // CHILD_TILE
    tile_rows = CHILD_TILE * group
    kv_width = kv_ref.shape[1] // kv_heads
    base_col = to_column(idx_ref[0:1, :].astype(f32)).astype(i32)
    srank_col = to_column(idx_ref[2:3, :].astype(f32)).astype(i32)
    unsort = onehot(srank_col == iota((children, children), 1))
    contexts, values = [], []
    for g in range(kv_heads):
        take = onehot(iota((children, rows), 1) == base_col + g * capacity)
        got = dot(take, box_ref[...])
        stat = got[:, group * head_dim + kv_width :]
        for h in range(group):
            far_lse = stat[:, h : h + 1] + stat[:, 16 + h : 17 + h] + stat[:, 32 + h : 33 + h]
            share = got[:, h * head_dim : (h + 1) * head_dim]
            pick = [slice(t * tile_rows + h * CHILD_TILE, t * tile_rows + (h + 1) * CHILD_TILE) for t in range(tiles)]
            near = jnp.concatenate([o_ref[g, at, :] for at in pick], axis=0)
            near_lse = jnp.concatenate([lse_ref[g, at, :] for at in pick], axis=0)
            part = 1.0 / (1.0 + jnp.exp(far_lse - near_lse))
            rest = 1.0 / (1.0 + jnp.exp(near_lse - far_lse))
            contexts.append((near * part + share * rest).astype(bf16))
        values.append(got[:, group * head_dim : group * head_dim + kv_width].astype(bf16))
    ctx_ref[...] = dot(unsort, jnp.concatenate(contexts, axis=1)).astype(bf16)
    kv_ref[...] = dot(unsort, jnp.concatenate(values, axis=1)).astype(bf16)


def params(mib, **kw):
    return pltpu.CompilerParams(vmem_limit_bytes=mib * 2**20, **kw)


def shape(dims, dtype):
    return jax.ShapeDtypeStruct(dims, dtype)


def exchange(box, devices):
    rows, width = box.shape
    out = lax.all_to_all(
        box.reshape(devices, rows // devices, width), ("row", "col"), split_axis=0, concat_axis=0, tiled=True
    )
    return out.reshape(rows, width)


def local(child_parent, prefix_len, child_delta, parent_hidden, parent_cache, prefix_cache, norm_gain, w_query, w_kv):
    row_count, col_count = lax.axis_size("row"), lax.axis_size("col")
    devices = row_count * col_count
    children, features = child_delta.shape
    parents = parent_hidden.shape[0]
    capacity = 2 * ((children // (2 * col_count) + row_count - 1) // row_count)
    slots = devices * capacity
    parts = max(1, 8 // capacity)
    kv_heads, block, head_dim = parent_cache.shape[2], parent_cache.shape[3], parent_cache.shape[4]
    query_width = w_query.shape[1]
    half = query_width // kv_heads
    group = half // head_dim
    scale = 1.0 / math.sqrt(head_dim)
    box_count = slots * kv_heads

    box, idx, ids = pl.pallas_call(
        functools.partial(pack_kernel, parents, capacity, parts, slots),
        out_shape=(
            shape((slots * parts, features // parts), bf16),
            shape((8, children), i32),
            shape((1, slots), i32),
        ),
        in_specs=[VMEM] * 3,
        out_specs=(VMEM, VMEM, VMEM),
        compiler_params=params(12),
        name="pack",
    )(child_parent.reshape(1, children), prefix_len.reshape(1, children), child_delta)
    far_box = exchange(box, devices)
    far_ids = lax.all_to_all(
        ids.reshape(devices, capacity), ("row", "col"), split_axis=0, concat_axis=0, tiled=True
    ).reshape(1, slots)

    queries, query_box, new_kv = pl.pallas_call(
        functools.partial(project_kernel, capacity, parts),
        out_shape=(
            shape((slots, query_width), bf16),
            shape((box_count, half), bf16),
            shape((slots, w_kv.shape[1]), bf16),
        ),
        in_specs=[VMEM] * 6,
        out_specs=(VMEM, VMEM, VMEM),
        scratch_shapes=[pltpu.VMEM((slots, features), f32), pltpu.VMEM((slots, features), bf16)],
        compiler_params=params(32),
        name="project",
    )(far_box, far_ids, parent_hidden, norm_gain.reshape(1, features), w_query, w_kv)
    near_query = exchange(query_box, devices)

    share_width = half + w_kv.shape[1] // kv_heads + head_dim
    share_box = pl.pallas_call(
        functools.partial(parent_kernel, capacity, scale),
        out_shape=shape((box_count, share_width), bf16),
        in_specs=[SMEM, VMEM, VMEM, VMEM],
        out_specs=VMEM,
        scratch_shapes=[pltpu.VMEM((kv_heads, slots * 8, head_dim), f32)] * 3,
        compiler_params=params(16),
        name="parent_attend",
    )(far_ids, queries, new_kv, parent_cache)
    near_share = exchange(share_box, devices)

    tile_rows = CHILD_TILE * group
    near, near_lse = pl.pallas_call(
        functools.partial(prefix_kernel, capacity, scale * LOG2E, block),
        out_shape=(
            shape((kv_heads, children * group, head_dim), f32),
            shape((kv_heads, children * group, head_dim), f32),
        ),
        in_specs=[SMEM, VMEM, VMEM, VMEM],
        out_specs=(VMEM, VMEM),
        scratch_shapes=[pltpu.VMEM((kv_heads, children * group, head_dim), bf16)]
        + [pltpu.VMEM((kv_heads, tile_rows, head_dim), f32)] * 3,
        compiler_params=params(20),
        name="prefix_attend",
    )(idx, idx, near_query, prefix_cache[0])

    return pl.pallas_call(
        functools.partial(merge_kernel, capacity),
        out_shape=(shape((children, query_width), bf16), shape((children, w_kv.shape[1]), bf16)),
        in_specs=[VMEM] * 4,
        out_specs=(VMEM, VMEM),
        compiler_params=params(16),
        name="merge",
    )(idx, near_share, near, near_lse)


def solution(mesh):
    spec = ("row", "col")
    return jax.shard_map(
        local,
        mesh=mesh,
        in_specs=(
            P(spec),
            P(spec),
            P(spec, None),
            P(spec, None),
            P(spec, None, None, None, None),
            P(spec, None, None, None, None),
            P(),
            P(),
            P(),
        ),
        out_specs=(P(spec, None), P(spec, None)),
        check_vma=False,
    )
```

time: 244 us -> 161 us (0.66)
  Pallas kernels: 0 us -> 93.1 us
  matrix products: 61.4 us -> 0 us
  waiting for transfers between devices: 61.4 us -> 21.9 us
  blocking collectives: 43.6 us -> 14.3 us
  other arithmetic: 21.4 us -> 1.35 us
  local copies, waits for them, and re-layouts: 31.6 us -> 16.2 us
  starting transfers between devices: 23 us -> 12 us
    pallas_call x0 -> x5, Pallas kernels: none -> 93.1 us  [the longest x1 63.4 us: local(): pl.pallas_call(functools.partial(parent_kernel, capacity, scale), out_sha...]
    dot_general x6 -> x0, matrix products: 61.4 us -> none  [the longest x1 18.4 us: local(): jnp.einsum('hcgl,hld->chgd', weight_pre, prefix_rows[1], preferred_elemen...]
    all_gather x1 -> x0, blocking collectives: 43.6 us -> none  [local(): whole_map = lax.all_gather(child_parent, ('row', 'col'), axis=0, tiled=True)]
    all_to_all x7 -> x3, waiting for transfers between devices: 61.4 us -> 21.9 us  [exchange(): lax.all_to_all(box.reshape(devices, rows // devices, width), ('row', 'col...]
    reduce_sum x5 -> x0, other arithmetic: 20.6 us -> none  [the longest x1 16.8 us: local(): sum_pre = jnp.sum(jnp.exp(score_pre - top_pre), axis=-1, keepdims=True)]
    gather x10 -> x0, local copies, waits for them, and re-layouts: 16.7 us -> none  [the longest x1 10.6 us: local(): own_blocks = parent_cache[send_ids.reshape(-1)]]
    all_to_all x0 -> x1, blocking collectives: none -> 14.3 us  [local(): lax.all_to_all(ids.reshape(devices, capacity), ('row', 'col'), split_axis...]
    unnamed x13 -> x16, local copies, waits for them, and re-layouts: 1.02 us -> 14.8 us
  transfers between devices with their start and end apart: 7 -> 3, of which waited for: 6 -> 1; matrix products, arithmetic and copies ran while one was open for 13% -> 1% of each run, Pallas kernels for 0% -> 54%
where the time goes in v1:
time: 161 us; the launch traced here: 160 us
  Pallas kernels  93.1 us (58%)
  waiting for transfers between devices  21.9 us (14%)
  local copies, waits for them, and re-layouts  16.2 us (10%)
  blocking collectives  14.3 us (9%)
  starting transfers between devices  12 us (7%)
    pallas_call x1, Pallas kernels, local(): pl.pallas_call(functools.partial(parent_kernel, capacity, scale), out_sha...  63.4 us
    pallas_call x1, Pallas kernels, local(): pl.pallas_call(functools.partial(prefix_kernel, capacity, scale * LOG2E,...  22.2 us
    all_to_all x3, waiting for transfers between devices, exchange(): lax.all_to_all(box.reshape(devices, rows // devices, width), ('row', 'col...  21.9 us
    unnamed x16, local copies, waits for them, and re-layouts  14.8 us
    all_to_all x1, blocking collectives, local(): lax.all_to_all(ids.reshape(devices, capacity), ('row', 'col'), split_axis...  14.3 us
    all_to_all x3, starting transfers between devices, exchange(): lax.all_to_all(box.reshape(devices, rows // devices, width), ('row', 'col...  12 us
    pallas_call x1, Pallas kernels, local(): pl.pallas_call(functools.partial(project_kernel, capacity, parts), out_sh...  4.09 us
  transfers between devices with their start and end apart: 3, of which 1 were waited for; matrix products, arithmetic and copies ran while one was open for 1% of the time, Pallas kernels for 54%

profile of v1, /device:TPU:0, one launch (start us, length us, event | category | flops | bytes accessed | tf_op | source)
XLA Modules:
  0.0 159.5 jit_solution(13870383887751100327)
XLA Ops:
  0.6 1.2 copy-done.4
  1.8 0.7 copy-done.6
  2.5 0.7 copy-done.7
  3.1 1.4 pack.1
  4.5 0.5 broadcast.6
  5.1 0.7 reduce.6
  5.7 0.1 all_to_all.15
  5.8 14.3 %all_to_all.24 = s32[32,1,4]{2,1,0:T(1,128)S(1)} all-to-all(s32[32,1,4]{2,1,0:T(1,128)S(1)} %bitcast.16), channel_id=1, replica_groups=mesh['row'=8,'col'=4] {'row','col'}, dimensions={0} | all-to-all | bytes 1024 | tf_op jit(solution)/shard_map/all_to_all | solution.py:318
  20.1 2.6 %all-to-all-start.1 = ((bf16[32,8,1792]{2,1,0:T(8,128)(2,1)}), bf16[32,8,1792]{2,1,0:T(8,128)(2,1)S(1)}, u32[]{:S(2)}, u32[]{:S(2)}) async-start(bf16[32,8,1792]{2,1,0:T(8,128)(2,1)} %bitcast.3), calls=%async_computation.1 | async-start | bytes 1835008 | tf_op jit(solution)/shard_map/all_to_all | solution.py:284
  22.8 0.7 reshape.44.gain_ref
  23.5 0.7 reduce.7
  24.2 0.1 reshape.41.ids_ref
  24.3 21.8 %all-to-all-done.1 = bf16[32,8,1792]{2,1,0:T(8,128)(2,1)S(1)} async-done(((bf16[32,8,1792]{2,1,0:T(8,128)(2,1)}), bf16[32,8,1792]{2,1,0:T(8,128)(2,1)S(1)}, u32[]{:S(2)}, u32[]{:S(2)}) %all-to-all-start.1) | async-done | bytes 917536 | tf_op jit(solution)/shard_map/all_to_all | solution.py:284
  46.2 4.6 %copy-done = bf16[3584,1792]{1,0:T(8,128)(2,1)S(1)} copy-done((bf16[3584,1792]{1,0:T(8,128)(2,1)S(1)}, bf16[3584,1792]{1,0:T(8,128)(2,1)}, u32[]{:S(2)}) %copy-start) | copy-done | bytes 12845080
  50.8 2.0 %copy-done.3 = bf16[3584,512]{1,0:T(8,128)(2,1)S(1)} copy-done((bf16[3584,512]{1,0:T(8,128)(2,1)S(1)}, bf16[3584,512]{1,0:T(8,128)(2,1)}, u32[]{:S(2)}) %copy-start.3) | copy-done | bytes 3670040
  52.9 0.9 copy-done.5
  53.8 4.1 %project.1 = (bf16[128,1792]{1,0:T(8,128)(2,1)S(1)}, bf16[256,896]{1,0:T(8,128)(2,1)}, bf16[128,512]{1,0:T(8,128)(2,1)S(1)}) custom-call(bf16[256,1792]{1,0:T(8,128)(2,1)S(1)} %bitcast.11, s32[1,128]{1,0:T(1,128)S(1)} %reshape.41.ids_ref, bf16[32,3584]{1,0:T(8,128)(2,1)S(1)} %copy-done.5, f32[1,3584]{1,0:T(1,128)S(1)} %reshape.44.gain_ref, ...), custom_call_target="tpu_custom_call" | custom-call | tf_op jit(solution)/shard_map/project/pallas_call | solution.py:322
  57.9 3.5 %all-to-all-start.3 = ((bf16[32,8,896]{2,1,0:T(8,128)(2,1)}), bf16[32,8,896]{2,1,0:T(8,128)(2,1)S(1)}, u32[]{:S(2)}, u32[]{:S(2)}) async-start(bf16[32,8,896]{2,1,0:T(8,128)(2,1)} %bitcast.7), calls=%async_computation.3 | async-start | bytes 917504 | tf_op jit(solution)/shard_map/all_to_all | solution.py:284
  61.5 2.2 %copy-done.2 = bf16[32,2,2,128,128]{4,3,2,1,0:T(8,128)(2,1)S(1)} copy-done((bf16[32,2,2,128,128]{4,3,2,1,0:T(8,128)(2,1)S(1)}, bf16[32,2,2,128,128]{4,3,2,1,0:T(8,128)(2,1)}, u32[]{:S(2)}) %copy-start.2) | copy-done | bytes 4194328
  63.6 63.4 %parent_attend.1 = bf16[256,1280]{1,0:T(8,128)(2,1)} custom-call(s32[1,128]{1,0:T(1,128)S(1)} %reshape.41.ids_ref, bf16[128,1792]{1,0:T(8,128)(2,1)S(1)} %get-tuple-element.13.q_ref, bf16[128,512]{1,0:T(8,128)(2,1)S(1)} %get-tuple-element.14.kv_ref, bf16[32,2,2,128,128]{4,3,2,1,0:T(8,128)(2,1)S(1)} %copy-done.2), custom_call_target="tpu_custom_call" | custom-call | tf_op jit(solution)/shard_map/parent_attend/pallas_call | solution.py:338
  127.0 5.8 %all-to-all-start.2 = ((bf16[32,8,1280]{2,1,0:T(8,128)(2,1)}), bf16[32,8,1280]{2,1,0:T(8,128)(2,1)S(1)}, u32[]{:S(2)}, u32[]{:S(2)}) async-start(bf16[32,8,1280]{2,1,0:T(8,128)(2,1)} %bitcast.5), calls=%async_computation.2 | async-start | bytes 1310720 | tf_op jit(solution)/shard_map/all_to_all | solution.py:284
  132.8 2.5 %copy-done.1 = bf16[1,2,2,5120,128]{4,3,2,1,0:T(8,128)(2,1)S(1)} copy-done((bf16[1,2,2,5120,128]{4,3,2,1,0:T(8,128)(2,1)S(1)}, bf16[1,2,2,5120,128]{4,3,2,1,0:T(8,128)(2,1)}, u32[]{:S(2)}) %copy-start.1) | copy-done | bytes 5242904
  135.3 22.2 %prefix_attend.1 = (f32[2,896,128]{2,1,0:T(8,128)S(1)}, f32[2,896,128]{2,1,0:T(8,128)S(1)}) custom-call(s32[8,128]{1,0:T(8,128)S(1)} %get-tuple-element.10.idx_smem.idx_ref, s32[8,128]{1,0:T(8,128)S(1)} %get-tuple-element.10.idx_smem.idx_ref, bf16[256,896]{1,0:T(8,128)(2,1)S(1)} %bitcast.13, bf16[2,2,5120,128]{3,2,1,0:T(8,128)(2,1)S(1)} %bitcast.10), custom_call_target="tpu_custom_call" | custom-call | tf_op jit(solution)/shard_map/prefix_attend/pallas_call | solution.py:350
  157.6 2.0 %merge.1 = (bf16[128,1792]{1,0:T(8,128)(2,1)}, bf16[128,512]{1,0:T(8,128)(2,1)}) custom-call(s32[8,128]{1,0:T(8,128)S(1)} %get-tuple-element.10.idx_smem.idx_ref, bf16[256,1280]{1,0:T(8,128)(2,1)S(1)} %bitcast.12, f32[2,896,128]{2,1,0:T(8,128)S(1)} %get-tuple-element.16.o_ref, f32[2,896,128]{2,1,0:T(8,128)S(1)} %get-tuple-element.17.lse_ref), custom_call_target="tpu_custom_call" | custom-call | tf_op jit(solution)/shard_map/merge/pallas_call | solution.py:364
  (10 shorter events, 0.0 us)
Async XLA Ops:
  0.6 1.2 copy-start.4
  1.8 0.7 copy-start.6
  2.5 0.7 copy-start.7
  20.1 26.0 %all-to-all-start.1 = ((bf16[32,8,1792]{2,1,0:T(8,128)(2,1)}), bf16[32,8,1792]{2,1,0:T(8,128)(2,1)S(1)}, u32[]{:S(2)}, u32[]{:S(2)}) async-start(bf16[32,8,1792]{2,1,0:T(8,128)(2,1)} %bitcast.3), calls=%async_computation.1 | async-start | bytes 1835008 | tf_op jit(solution)/shard_map/all_to_all | solution.py:284
  46.2 4.7 %copy-start = (bf16[3584,1792]{1,0:T(8,128)(2,1)S(1)}, bf16[3584,1792]{1,0:T(8,128)(2,1)}, u32[]{:S(2)}) copy-start(bf16[3584,1792]{1,0:T(8,128)(2,1)} %wq_ref.1) | copy-start | bytes 38535172
  50.8 2.0 %copy-start.3 = (bf16[3584,512]{1,0:T(8,128)(2,1)S(1)}, bf16[3584,512]{1,0:T(8,128)(2,1)}, u32[]{:S(2)}) copy-start(bf16[3584,512]{1,0:T(8,128)(2,1)} %wkv_ref.1) | copy-start | bytes 11010052
  52.9 0.9 copy-start.5
  57.9 69.1 %all-to-all-start.3 = ((bf16[32,8,896]{2,1,0:T(8,128)(2,1)}), bf16[32,8,896]{2,1,0:T(8,128)(2,1)S(1)}, u32[]{:S(2)}, u32[]{:S(2)}) async-start(bf16[32,8,896]{2,1,0:T(8,128)(2,1)} %bitcast.7), calls=%async_computation.3 | async-start | bytes 917504 | tf_op jit(solution)/shard_map/all_to_all | solution.py:284
  61.4 2.2 %copy-start.2 = (bf16[32,2,2,128,128]{4,3,2,1,0:T(8,128)(2,1)S(1)}, bf16[32,2,2,128,128]{4,3,2,1,0:T(8,128)(2,1)}, u32[]{:S(2)}) copy-start(bf16[32,2,2,128,128]{4,3,2,1,0:T(8,128)(2,1)} %cache_ref.1) | copy-start | bytes 12582916
  127.0 30.6 %all-to-all-start.2 = ((bf16[32,8,1280]{2,1,0:T(8,128)(2,1)}), bf16[32,8,1280]{2,1,0:T(8,128)(2,1)S(1)}, u32[]{:S(2)}, u32[]{:S(2)}) async-start(bf16[32,8,1280]{2,1,0:T(8,128)(2,1)} %bitcast.5), calls=%async_computation.2 | async-start | bytes 1310720 | tf_op jit(solution)/shard_map/all_to_all | solution.py:284
  132.8 2.5 %copy-start.1 = (bf16[1,2,2,5120,128]{4,3,2,1,0:T(8,128)(2,1)S(1)}, bf16[1,2,2,5120,128]{4,3,2,1,0:T(8,128)(2,1)}, u32[]{:S(2)}) copy-start(bf16[1,2,2,5120,128]{4,3,2,1,0:T(8,128)(2,1)} %param.14) | copy-start | bytes 15728644
